TPU v7x, 256 devices: a whole 4x4x8 slice. The times are simulated.
256 devices in a mesh: mkt: 32 (over z, y), draw: 8 (over x, core).
Axes of the slice: x: 4, y: 4, z: 8, core: 2. Of those that a mesh axis runs over, the one named last changes fastest.
Arguments:
- x_char: float32 [1536, 56, 8], P('mkt'), may hold values from -2.5 to 2.5
- nu_draws: float32 [1536, 8, 4096], P('mkt', None, 'draw'), may hold values from -3 to 3
- coef_sigma: float32 [8], replicated, may hold values from 0.3 to 1.2
- log_share: float32 [1536, 56], P('mkt'), may hold values from -7 to -4.5
- counts: int32 [1536], P('mkt'), may hold values from 28 to 56
Outputs:
- mean_util: float32 [1536, 56], P('mkt')
- jacobian: float32 [1536, 56, 56], P(('mkt', 'draw'))
- sup_norms: float32 [3], replicated
Inputs may be any that keep to these rules, and one draw needn't show every extreme that they name: Products 0 to counts - 1 of a market are valid; the other slots are padding.
All inputs are finite; a program needn't handle non-finite values. Where the computation divides by a largest or mean magnitude, that divisor is 1e-20 or more.
Results may differ from a plain program's by a relative error of at most 0.00013.
Values sent between devices are 32-bit elements; how exact they have to be, the bound alone decides.
No kernel may reach another device: no remote copies, remote signals or barrier semaphores. Data moves between devices by JAX's collectives and lax.ppermute only.
A program may use at most 64 MiB of HBM per device.

v0:
```python
import jax
import jax.numpy as jnp
import numpy as np
from jax import lax
from jax.sharding import PartitionSpec as P

ITERS = 3


step_cap = 0.25
epsilon = 1e-06


def copy_for_each(shard, axis):
    copies = jnp.broadcast_to(shard, (lax.axis_size(axis), *shard.shape))
    return lax.all_to_all(copies, axis, split_axis=0, concat_axis=0, tiled=True)


def over_copies(shard, axis):
    everything = copy_for_each(shard, axis)
    return jnp.sum(everything, axis=0)


def over_copies_2(shard, axis):
    return copy_for_each(shard, axis).max(axis=0)


def total_of_pieces(shard, axis):
    return lax.all_gather(shard, axis).sum(0)


def market_terms(mean_util, scaled, nu_draws, usable, inverse, with_products):
    tastes = jnp.einsum("mjk,mkr->mjr", scaled, nu_draws, precision=lax.Precision.HIGHEST)
    raised = jnp.where(usable[:, :, None], jnp.exp(mean_util[:, :, None] + tastes), 0.0)
    chance = raised / (1.0 + jnp.sum(raised, axis=1, keepdims=True))
    shares = jnp.sum(chance, axis=2) * inverse
    if with_products:
        cross_sums = (
            jnp.einsum("mjr,mlr->mjl", chance, chance, precision=lax.Precision.HIGHEST) * inverse
        )
        return (shares, cross_sums)
    return shares


def evaluate(mean_util, scaled, nu_draws, usable, inverse, with_products):
    groups = mean_util.shape[0] // 8
    folded = (
        mean_util.reshape(groups, 8, mean_util.shape[1]),
        scaled.reshape(groups, 8, scaled.shape[1], scaled.shape[2]),
        nu_draws.reshape(groups, 8, nu_draws.shape[1], nu_draws.shape[2]),
        usable.reshape(groups, 8, usable.shape[1]),
    )

    def per_group(items):
        return market_terms(items[0], items[1], items[2], items[3], inverse, with_products)

    def unfold(member):
        return member.reshape((groups * 8,) + member.shape[2:])

    return jax.tree.map(unfold, lax.map(per_group, folded))


def pack_cross(cross_part):
    slots = cross_part.shape[1]
    upper_rows, upper_cols = np.triu_indices(slots)
    flat_index = jnp.asarray((upper_rows * slots + upper_cols).astype(np.int32))
    return jnp.take(cross_part.reshape(cross_part.shape[0], slots * slots), flat_index, axis=1)


def unpack_cross(packed, slots):
    upper_rows, upper_cols = np.triu_indices(slots)
    lookup_table = np.zeros((slots, slots), np.int32)
    positions = np.arange(upper_rows.shape[0], dtype=np.int32)
    lookup_table[upper_rows, upper_cols] = positions
    lookup_table[upper_cols, upper_rows] = positions
    whole = jnp.take(packed, jnp.asarray(lookup_table.reshape(-1)), axis=1)
    return whole.reshape(packed.shape[0], slots, slots)


def prepare_cross(cross_part):
    return pack_cross(cross_part)


def restore_cross(summed, slots):
    return unpack_cross(summed, slots)


def contraction(log_share, shares, usable):
    return jnp.where(usable, log_share - jnp.log(jnp.where(usable, shares, 1.0)), 0.0)


def step_size(largest):
    return jnp.minimum(1.0, step_cap / (largest + epsilon))


def jacobian_rows(shares, cross_sums, usable):
    slots = shares.shape[1]
    divisor = jnp.where(usable, shares, 1.0)
    identity = jnp.eye(slots, dtype=jnp.float32)
    paired = usable[:, :, None] & usable[:, None, :]
    return jnp.where(paired, identity[None, :, :] - cross_sums / divisor[:, :, None], 0.0)


def whole_sweeps(
    mean_util, scaled, nu_draws, usable, log_share, inverse, total_fn, peak_fn, final_fn
):
    norms_list = []
    for sweep in range(ITERS):
        partial_value = evaluate(mean_util, scaled, nu_draws, usable, inverse, False)
        shares = total_fn(partial_value)
        change = contraction(log_share, shares, usable)
        largest = peak_fn(jnp.max(jnp.abs(change)))
        mean_util = mean_util + step_size(largest) * change
        norms_list.append(largest)
    partial_value, cross_part = evaluate(mean_util, scaled, nu_draws, usable, inverse, True)
    shares, summed = final_fn(partial_value, prepare_cross(cross_part))
    cross_sums = restore_cross(summed, cross_part.shape[1])
    return (mean_util, shares, cross_sums, norms_list)


def shards(x_char, nu_draws, coef_sigma, log_share, counts):
    slots = log_share.shape[1]
    markets = log_share.shape[0]
    draw_count = lax.axis_size("draw")
    inverse = 1.0 / (nu_draws.shape[2] * draw_count)
    usable = jnp.arange(slots, dtype=jnp.int32)[None, :] < counts[:, None]
    scaled = x_char * coef_sigma[None, None, :]
    inside = jnp.sum(jnp.where(usable, jnp.exp(log_share), 0.0), axis=1)
    mean_util = jnp.where(usable, log_share - jnp.log(1.0 - inside)[:, None], 0.0)
    own_rows = markets // draw_count
    first_row = lax.axis_index("draw") * own_rows
    usable_own = lax.dynamic_slice_in_dim(usable, first_row, own_rows, 0)

    def total_market(partial_value):
        return over_copies(partial_value, "draw")

    def peak_market(local):
        return over_copies_2(local, "mkt")

    def final_market(partial_value, cross_part):
        return (total_of_pieces(partial_value, "draw"), total_of_pieces(cross_part, "draw"))

    mean_util, shares, cross_sums, norms_list = whole_sweeps(
        mean_util,
        scaled,
        nu_draws,
        usable,
        log_share,
        inverse,
        total_market,
        peak_market,
        final_market,
    )
    jacobian = jacobian_rows(
        lax.dynamic_slice_in_dim(shares, first_row, own_rows, 0),
        lax.dynamic_slice_in_dim(cross_sums, first_row, own_rows, 0),
        usable_own,
    )
    return (mean_util, jacobian, jnp.stack(norms_list))


def solution(mesh):
    return jax.shard_map(
        shards,
        mesh=mesh,
        in_specs=(P("mkt", None, None), P("mkt", None, "draw"), P(), P("mkt", None), P("mkt")),
        out_specs=(P("mkt", None), P(("mkt", "draw"), None, None), P()),
        check_vma=False,
    )
```

profile of v0, /device:TPU:1, one launch (start us, length us, event | category | flops | bytes accessed | tf_op | source)
XLA Modules:
  0.0 202.1 jit_solution(15484794193982290934)
XLA Ops:
  10.8 13.2 %while.42 = (s32[]{:T(128)}, f32[6,8,56]{2,1,0:T(8,128)S(1)}, pred[6,8,56]{2,1,0:T(8,128)(4,1)S(1)}, f32[6,8,56]{2,1,0:T(8,128)S(1)}, f32[6,8,56,8]{2,3,1,0:T(8,128)S(1)}, /*index=5*/f32[6,8,8,512]{3,2,1,0:T(8,128)}, s32[]{:T(128)}) while((s32[]{:T(128)}, f32[6,8,56]{2,1,0:T(8,128)S(1)}, pred[6,8,56]{2,1,0:T(8,128)(4,1)S(1)}, ...), condition=%wide.region_4.5_spmd, body=%wide.region_1.4_spmd.sunk | while | flops 23166976 | bytes 2085081 | solution.py:60
  10.8 2.0 fusion.44
  13.0 2.0 fusion.44
  15.2 2.0 fusion.44
  17.4 2.0 fusion.44
  19.6 2.0 fusion.44
  21.8 2.0 fusion.44
  24.2 10.5 %all_to_all.33 = f32[8,1,2688]{2,1,0:T(1,128)S(1)} all-to-all(f32[8,1,2688]{2,1,0:T(1,128)S(1)} %reshape.212), channel_id=1, replica_groups=mesh['mkt'=32,'draw'=8] {'draw'}, dimensions={0} | all-to-all | bytes 172032 | tf_op jit(solution)/shard_map/all_to_all | solution.py:16
  38.2 11.2 %all-to-all-start.1 = ((f32[32,1,1]{2,1,0:T(1,128)}), f32[32,1,1]{2,1,0:T(1,128)S(1)}, u32[]{:S(2)}, u32[]{:S(2)}) async-start(f32[32,1,1]{2,1,0:T(1,128)} %broadcast_in_dim.144), calls=%async_computation.1 | async-start | bytes 32768 | tf_op jit(solution)/shard_map/all_to_all | solution.py:16
  49.5 8.5 %all-to-all-done.1 = f32[32,1,1]{2,1,0:T(1,128)S(1)} async-done(((f32[32,1,1]{2,1,0:T(1,128)}), f32[32,1,1]{2,1,0:T(1,128)S(1)}, u32[]{:S(2)}, u32[]{:S(2)}) %all-to-all-start.1) | async-done | bytes 160 | tf_op jit(solution)/shard_map/all_to_all | solution.py:16
  59.5 13.1 %while.43 = (s32[]{:T(128)}, f32[6,8,56]{2,1,0:T(8,128)S(1)}, pred[6,8,56]{2,1,0:T(8,128)(4,1)S(1)}, f32[6,8,56]{2,1,0:T(8,128)S(1)}, f32[6,8,56,8]{2,3,1,0:T(8,128)S(1)}, /*index=5*/f32[6,8,8,512]{3,2,1,0:T(8,128)}, s32[]{:T(128)}) while((s32[]{:T(128)}, f32[6,8,56]{2,1,0:T(8,128)S(1)}, pred[6,8,56]{2,1,0:T(8,128)(4,1)S(1)}, ...), condition=%wide.region_11.12_spmd, body=%wide.region_8.11_spmd.sunk | while | flops 23166976 | bytes 2085081 | solution.py:60
  59.6 2.0 fusion.45
  61.7 2.0 fusion.45
  66.1 2.0 fusion.45
  70.5 2.0 fusion.45
  72.9 9.5 %all_to_all.34 = f32[8,1,2688]{2,1,0:T(1,128)S(1)} all-to-all(f32[8,1,2688]{2,1,0:T(1,128)S(1)} %reshape.214), channel_id=1, replica_groups=mesh['mkt'=32,'draw'=8] {'draw'}, dimensions={0} | all-to-all | bytes 172032 | tf_op jit(solution)/shard_map/all_to_all | solution.py:16
  85.4 3.8 %all-to-all-start.3 = ((f32[32,1,1]{2,1,0:T(1,128)}), f32[32,1,1]{2,1,0:T(1,128)S(1)}, u32[]{:S(2)}, u32[]{:S(2)}) async-start(f32[32,1,1]{2,1,0:T(1,128)} %broadcast_in_dim.146), calls=%async_computation.3 | async-start | bytes 32768 | tf_op jit(solution)/shard_map/all_to_all | solution.py:16
  89.3 8.5 %all-to-all-done.3 = f32[32,1,1]{2,1,0:T(1,128)S(1)} async-done(((f32[32,1,1]{2,1,0:T(1,128)}), f32[32,1,1]{2,1,0:T(1,128)S(1)}, u32[]{:S(2)}, u32[]{:S(2)}) %all-to-all-start.3) | async-done | bytes 160 | tf_op jit(solution)/shard_map/all_to_all | solution.py:16
  99.1 13.1 %while.44 = (s32[]{:T(128)}, f32[6,8,56]{2,1,0:T(8,128)S(1)}, pred[6,8,56]{2,1,0:T(8,128)(4,1)S(1)}, f32[6,8,56]{2,1,0:T(8,128)S(1)}, f32[6,8,56,8]{2,3,1,0:T(8,128)S(1)}, /*index=5*/f32[6,8,8,512]{3,2,1,0:T(8,128)}, s32[]{:T(128)}) while((s32[]{:T(128)}, f32[6,8,56]{2,1,0:T(8,128)S(1)}, pred[6,8,56]{2,1,0:T(8,128)(4,1)S(1)}, ...), condition=%wide.region_18.19_spmd, body=%wide.region_15.18_spmd.sunk | while | flops 23166976 | bytes 2085081 | solution.py:60
  99.1 2.0 fusion.46
  103.5 2.0 fusion.46
  107.9 2.0 fusion.46
  112.5 9.3 %all_to_all.35 = f32[8,1,2688]{2,1,0:T(1,128)S(1)} all-to-all(f32[8,1,2688]{2,1,0:T(1,128)S(1)} %reshape.216), channel_id=1, replica_groups=mesh['mkt'=32,'draw'=8] {'draw'}, dimensions={0} | all-to-all | bytes 172032 | tf_op jit(solution)/shard_map/all_to_all | solution.py:16
  124.7 3.8 %all-to-all-start.5 = ((f32[32,1,1]{2,1,0:T(1,128)}), f32[32,1,1]{2,1,0:T(1,128)S(1)}, u32[]{:S(2)}, u32[]{:S(2)}) async-start(f32[32,1,1]{2,1,0:T(1,128)} %broadcast_in_dim.148), calls=%async_computation.5 | async-start | bytes 32768 | tf_op jit(solution)/shard_map/all_to_all | solution.py:16
  128.7 8.5 %all-to-all-done.5 = f32[32,1,1]{2,1,0:T(1,128)S(1)} async-done(((f32[32,1,1]{2,1,0:T(1,128)}), f32[32,1,1]{2,1,0:T(1,128)S(1)}, u32[]{:S(2)}, u32[]{:S(2)}) %all-to-all-start.5) | async-done | bytes 160 | tf_op jit(solution)/shard_map/all_to_all | solution.py:16
  138.6 19.0 %while.45 = (s32[]{:T(128)}, f32[6,8,56]{2,1,0:T(8,128)S(1)}, f32[6,8,56,56]{3,2,1,0:T(8,128)S(1)}, pred[6,8,56]{2,1,0:T(8,128)(4,1)S(1)}, f32[6,8,56]{2,1,0:T(8...) while((s32[]{:T(128)}, f32[6,8,56]{2,1,0:T(8,128)S(1)}, ...), condition=%wide.region_25.26_spmd, body=%wide.region_22.25_spmd.sunk | while | flops 177562112 | bytes 3248357 | solution.py:60
  151.3 2.0 fusion.47
  158.5 3.2 %gather_fusion = f32[1596,48]{1,0:T(8,128)S(1)} fusion(f32[48,3136]{0,1:T(8,128)S(1)} %copy.26, s32[2048]{0:T(1024)S(1)} %pad_clamp_fusion.1), kind=kCustom, calls=%fused_computation | custom fusion | bytes 619248 | tf_op jit(solution)/shard_map/jit(_take)/gather | solution.py:67
  162.9 15.0 %all_gather.8 = f32[8,48,56]{2,1,0:T(8,128)S(1)} all-gather(f32[1,48,56]{2,1,0:T(8,128)S(1)} %bitcast.140), channel_id=1, replica_groups=mesh['mkt'=32,'draw'=8] {'draw'}, dimensions={0}, use_global_device_ids=true | all-gather | bytes 96768 | tf_op jit(solution)/shard_map/all_gather | solution.py:29
  177.9 2.5 %pad_maximum_fusion = f32[3]{0:T(128)} fusion(f32[1]{0:T(128)} %bitcast.37, f32[1]{0:T(128)} %bitcast.36, f32[1]{0:T(128)} %bitcast.35), kind=kLoop, calls=%fused_computation.82 | loop fusion | flops 6 | bytes 24 | tf_op jit(solution)/shard_map/stack | solution.py:159
  180.3 5.3 %all-gather.3.cloned.1.call-done = f32[384,1596]{1,0:T(8,128)} async-done(((f32[48,1596]{1,0:T(8,128)}), f32[384,1596]{1,0:T(8,128)}) %all-gather.3.cloned.1.call-update) | async-done | bytes 2451472 | tf_op jit(solution)/shard_map/all_gather | solution.py:29
  187.8 5.5 %gather_fusion.1 = f32[3136,48]{1,0:T(8,128)S(1)} fusion(f32[48,1596]{0,1:T(8,128)S(1)} %copy.28, s32[4096]{0:T(1024)S(1)} %pad_clamp_fusion), kind=kCustom, calls=%fused_computation.1 | custom fusion | bytes 1216768 | tf_op jit(solution)/shard_map/jit(_take)/gather | solution.py:76
  (202 shorter events, 51.6 us)
Async XLA Ops:
  10.8 25.5 %copy-start = (f32[48,56]{1,0:T(8,128)S(1)}, f32[48,56]{1,0:T(8,128)}, u32[]{:S(2)}) copy-start(f32[48,56]{1,0:T(8,128)} %param.18) | copy-start | bytes 32260
  10.8 25.5 %copy-start.2 = (s32[48]{0:T(128)S(1)}, s32[48]{0:T(128)}, u32[]{:S(2)}) copy-start(s32[48]{0:T(128)} %param.19) | copy-start | bytes 580
  38.2 19.8 %all-to-all-start.1 = ((f32[32,1,1]{2,1,0:T(1,128)}), f32[32,1,1]{2,1,0:T(1,128)S(1)}, u32[]{:S(2)}, u32[]{:S(2)}) async-start(f32[32,1,1]{2,1,0:T(1,128)} %broadcast_in_dim.144), calls=%async_computation.1 | async-start | bytes 32768 | tf_op jit(solution)/shard_map/all_to_all | solution.py:16
  85.4 12.4 %all-to-all-start.3 = ((f32[32,1,1]{2,1,0:T(1,128)}), f32[32,1,1]{2,1,0:T(1,128)S(1)}, u32[]{:S(2)}, u32[]{:S(2)}) async-start(f32[32,1,1]{2,1,0:T(1,128)} %broadcast_in_dim.146), calls=%async_computation.3 | async-start | bytes 32768 | tf_op jit(solution)/shard_map/all_to_all | solution.py:16
  99.1 29.5 %copy-start.4 = (s32[1596]{0:T(1024)S(1)}, s32[1596]{0:T(1024)}, u32[]{:S(2)}) copy-start(s32[1596]{0:T(1024)} %constant.151) | copy-start | bytes 19156
  124.7 12.4 %all-to-all-start.5 = ((f32[32,1,1]{2,1,0:T(1,128)}), f32[32,1,1]{2,1,0:T(1,128)S(1)}, u32[]{:S(2)}, u32[]{:S(2)}) async-start(f32[32,1,1]{2,1,0:T(1,128)} %broadcast_in_dim.148), calls=%async_computation.5 | async-start | bytes 32768 | tf_op jit(solution)/shard_map/all_to_all | solution.py:16
  128.6 57.1 %all-gather.3.cloned.1.call-start = ((), (), s32[]{:S(2)}) async-start(), calls=%async_computation.6 | async-start | bytes 2875392 | tf_op jit(solution)/shard_map/all_gather | solution.py:29
  157.6 0.9 copy-start.1
  158.5 4.3 %copy-start.3 = (s32[3136]{0:T(1024)S(1)}, s32[3136]{0:T(1024)}, u32[]{:S(2)}) copy-start(s32[3136]{0:T(1024)} %constant.152) | copy-start | bytes 37636
Sparse Core Ops, SparseCore 0:
  162.9 22.7 all-gather.2
where the time goes:
time: 203 us; the launch traced here: 202 us
  matrix products  52.9 us (26%)
  blocking collectives  44.3 us (22%)
  waiting for transfers between devices  30.9 us (15%)
  starting transfers between devices  18.9 us (9%)
  other arithmetic  18.7 us (9%)
  local copies, waits for them, and re-layouts  18.6 us (9%)
  between operations  16.5 us (8%)
    dot_general x24, matrix products, market_terms(): jnp.einsum('mjk,mkr->mjr', scaled, nu_draws, precision=lax.Precision.HIGH...  47 us
    all_to_all x3, blocking collectives, copy_for_each(): return lax.all_to_all(copies, axis, split_axis=0, concat_axis=0, tiled=True)  29.3 us
    all_to_all x3, waiting for transfers between devices, copy_for_each(): return lax.all_to_all(copies, axis, split_axis=0, concat_axis=0, tiled=True)  25.5 us
    all_to_all x3, starting transfers between devices, copy_for_each(): return lax.all_to_all(copies, axis, split_axis=0, concat_axis=0, tiled=True)  18.9 us
    all_gather x1, blocking collectives, total_of_pieces(): return lax.all_gather(shard, axis).sum(0)  15 us
    dot_general x6, matrix products, market_terms(): jnp.einsum('mjr,mlr->mjl', chance, chance, precision=lax.Precision.HIGHEST)  5.87 us
    gather x1, local copies, waits for them, and re-layouts, unpack_cross(): whole = jnp.take(packed, jnp.asarray(lookup_table.reshape(-1)), axis=1)  5.54 us
    all_gather x1, waiting for transfers between devices, total_of_pieces(): return lax.all_gather(shard, axis).sum(0)  5.34 us
  transfers between devices with their start and end apart: 4, of which 4 were waited for; matrix products, arithmetic and copies ran while one was open for 1% of the time, Pallas kernels for 0%

commit v1 on v0

v1 whole, which is shorter than its diff:
```python
import jax
import jax.numpy as jnp
from jax import lax
from jax.experimental import pallas as pl
from jax.experimental.pallas import tpu as pltpu
from jax.sharding import PartitionSpec as P

step_cap = 0.25
epsilon = 1e-06
LOG2E = 1.4426950408889634
VMEM = pl.BlockSpec(memory_space=pltpu.VMEM)
SMEM = pl.BlockSpec(memory_space=pltpu.SMEM)
EVERY = ("mkt", "draw")


def pieces(value):
    high = value.astype(jnp.bfloat16).astype(jnp.float32)
    rest = value - high
    middle = rest.astype(jnp.bfloat16).astype(jnp.float32)
    return high, middle, rest - middle


def first_market(own):
    return lax.axis_index("draw") * own


def fill(ref, value):
    tile = jnp.broadcast_to(value, (8, ref.shape[1]))
    for row in range(0, ref.shape[0], 8):
        ref[row : row + 8, :] = tile


def column(value, slot, lanes=128):
    return jnp.broadcast_to(value[:, slot : slot + 1], (value.shape[0], lanes))


def share_columns(weights, raised_ref, own):
    slots, width = weights.shape
    draws = raised_ref.shape[2]
    lane = lax.broadcasted_iota(jnp.int32, (slots, width), 1)
    totals = jnp.ones((slots, width), jnp.float32)
    for m in range(own):
        weight = column(weights, m)
        total = jnp.zeros((slots, 128), jnp.float32)
        for g in range(0, draws, 128):
            raised = raised_ref[m, :, g : g + 128]
            below = 1.0 + jnp.sum(raised * weight, axis=0, keepdims=True)
            total = total + raised * (1.0 / below)
        totals = jnp.where(lane == m, jnp.sum(total, axis=1, keepdims=True), totals)
    return totals * weights * (1.0 / draws)


def contraction(state_ref, mean_util, raised_ref, own):
    log_share, usable = state_ref[0], state_ref[1] > 0.0
    weights = jnp.where(usable, jnp.exp(mean_util), 0.0)
    shares = share_columns(weights, raised_ref, own)
    return jnp.where(usable, log_share - jnp.log(jnp.where(usable, shares, 1.0)), 0.0)


def start_kernel(own, counts_ref, sigma_ref, log_share_ref, x_ref, nu_ref, raised_ref, state_ref, peak_ref, rows_ref):
    base = first_market(own)
    slots = log_share_ref.shape[1]
    depth = x_ref.shape[1]
    span = nu_ref.shape[2]
    level = lax.broadcasted_iota(jnp.int32, (depth, slots), 0)
    sigma = jnp.zeros((depth, slots), jnp.float32)
    for k in range(depth):
        sigma = jnp.where(level == k, sigma_ref[k], sigma)
    for m in range(own):
        high, middle, low = pieces(x_ref[base + m] * sigma * LOG2E)
        left = jnp.concatenate([high, high, middle, high, low, middle], axis=0)
        left = jnp.transpose(left).astype(jnp.bfloat16)
        for s in range(nu_ref.shape[0] // own):
            high, middle, low = pieces(nu_ref[s * own + m])
            right = jnp.concatenate([high, middle, high, low, high, middle], axis=0)
            tastes = jnp.dot(left, right.astype(jnp.bfloat16), preferred_element_type=jnp.float32)
            raised_ref[m, :, s * span : (s + 1) * span] = jnp.exp2(tastes)
    rows_ref[...] = jnp.zeros_like(rows_ref)
    for m in range(own):
        rows_ref[m : m + 1, 0:slots] = log_share_ref[pl.ds(base + m, 1), :]
    log_share = jnp.transpose(rows_ref[...])[0:slots, :]
    slot = lax.broadcasted_iota(jnp.int32, (slots, 8), 0)
    lane = lax.broadcasted_iota(jnp.int32, (slots, 8), 1)
    count = jnp.zeros((slots, 8), jnp.int32)
    for m in range(own):
        count = jnp.where(lane == m, counts_ref[base + m], count)
    usable = slot < count
    inside = jnp.sum(jnp.where(usable, jnp.exp(log_share), 0.0), axis=0, keepdims=True)
    mean_util = jnp.where(usable, log_share - jnp.log(1.0 - inside), 0.0)
    state_ref[0] = log_share
    state_ref[1] = jnp.where(usable, 1.0, 0.0)
    state_ref[2] = mean_util
    change = contraction(state_ref, mean_util, raised_ref, own)
    state_ref[3] = change
    state_ref[4] = jnp.zeros_like(change)
    fill(peak_ref, jnp.max(jnp.abs(change)))


def moved(peaks_ref, state_ref):
    largest = jnp.max(peaks_ref[...])
    step = jnp.minimum(1.0, step_cap / (largest + epsilon))
    return largest, state_ref[2] + step * state_ref[3]


def norm_row(turn, largest, state_ref):
    row = lax.broadcasted_iota(jnp.int32, state_ref.shape[1:], 0)
    return jnp.where(row == turn, largest, state_ref[4])


def next_kernel(own, turn, peaks_ref, state_ref, raised_ref, out_ref, peak_ref):
    largest, mean_util = moved(peaks_ref, state_ref)
    change = contraction(state_ref, mean_util, raised_ref, own)
    out_ref[0] = state_ref[0]
    out_ref[1] = state_ref[1]
    out_ref[2] = mean_util
    out_ref[3] = change
    out_ref[4] = norm_row(turn, largest, state_ref)
    fill(peak_ref, jnp.max(jnp.abs(change)))


def settle_kernel(own, turn, peaks_ref, state_ref, out_ref, copies_ref, norms_ref):
    largest, mean_util = moved(peaks_ref, state_ref)
    out_ref[...] = mean_util
    norms = norm_row(turn, largest, state_ref)
    for t in range(turn + 1):
        norms_ref[t] = jnp.max(norms[t : t + 1, :])
    slots = mean_util.shape[0]
    padded = jnp.concatenate([mean_util, jnp.zeros((128 - slots, 8), jnp.float32)], axis=0)
    rows = jnp.transpose(padded)
    for d in range(copies_ref.shape[0]):
        copies_ref[d] = rows


def final_kernel(own, counts_ref, mean_ref, raised_ref, jacobian_ref, high_ref, both_ref):
    base = first_market(own)
    mean_util = mean_ref[...]
    slots = mean_util.shape[0]
    draws = raised_ref.shape[2]
    padding = jnp.zeros((64 - slots, 128), jnp.float32)
    row = lax.broadcasted_iota(jnp.int32, (slots, slots), 0)
    col = lax.broadcasted_iota(jnp.int32, (slots, slots), 1)
    slot = lax.broadcasted_iota(jnp.int32, (slots, 128), 0)
    for m in range(own):
        count = counts_ref[base + m]
        weight = jnp.where(slot < count, jnp.exp(column(mean_util, m)), 0.0)
        total = jnp.zeros((slots, 128), jnp.float32)
        buffer = m % 2
        for g in range(0, draws, 128):
            raised = raised_ref[m, :, g : g + 128] * weight
            chance = raised * (1.0 / (1.0 + jnp.sum(raised, axis=0, keepdims=True)))
            total = total + chance
            padded = jnp.concatenate([chance, padding], axis=0)
            high = padded.astype(jnp.bfloat16)
            low = (padded - high.astype(jnp.float32)).astype(jnp.bfloat16)
            both_ref[buffer, 0:64, g : g + 128] = high
            both_ref[buffer, 64:128, g : g + 128] = low
        product = lax.dot_general(
            both_ref[buffer, 0:64, :],
            both_ref[buffer],
            (((1,), (1,)), ((), ())),
            preferred_element_type=jnp.float32,
        )
        crossed = product[:, 64:128]
        cross = (product[:, 0:64] + crossed + jnp.transpose(crossed))[0:slots, 0:slots]
        shares = jnp.sum(total, axis=1, keepdims=True)
        divisor = jnp.where(row < count, shares, 1.0)
        identity = jnp.where(row == col, 1.0, 0.0)
        jacobian_ref[m] = jnp.where((row < count) & (col < count), identity - cross / divisor, 0.0)


def params(mebibytes=16):
    return pltpu.CompilerParams(vmem_limit_bytes=mebibytes << 20)


def shards(x_char, nu_draws, coef_sigma, log_share, counts):
    markets, slots = log_share.shape
    depth, span = nu_draws.shape[1:]
    draw_count, every = lax.axis_size("draw"), lax.axis_size(EVERY)
    own = markets // draw_count
    f32 = jnp.float32
    raised_shape = jax.ShapeDtypeStruct((own, slots, span * draw_count), f32)
    state_shape = jax.ShapeDtypeStruct((5, slots, 8), f32)
    peak_shape = jax.ShapeDtypeStruct((every, 128), f32)

    def everywhere(peak):
        return lax.all_to_all(peak.reshape(every, 1, 128), EVERY, 0, 0, tiled=True).reshape(every, 128)

    nu_own = lax.all_to_all(nu_draws, "draw", 0, 0, tiled=True)
    raised, state, peak = pl.pallas_call(
        lambda *refs: start_kernel(own, *refs),
        out_shape=(raised_shape, state_shape, peak_shape),
        in_specs=[SMEM, SMEM, VMEM, VMEM, VMEM],
        out_specs=(VMEM, VMEM, VMEM),
        scratch_shapes=[pltpu.VMEM((8, 128), f32)],
        compiler_params=params(),
        name="start",
    )(counts, coef_sigma, log_share, jnp.transpose(x_char, (0, 2, 1)), nu_own)
    for turn in range(2):
        state, peak = pl.pallas_call(
            lambda *refs, turn=turn: next_kernel(own, turn, *refs),
            out_shape=(state_shape, peak_shape),
            in_specs=[VMEM, VMEM, VMEM],
            out_specs=(VMEM, VMEM),
            compiler_params=params(),
            name="next",
        )(everywhere(peak), state, raised)
    mean_own, copies, norms = pl.pallas_call(
        lambda *refs: settle_kernel(own, 2, *refs),
        out_shape=(
            jax.ShapeDtypeStruct((slots, 8), f32),
            jax.ShapeDtypeStruct((draw_count, 8, 128), f32),
            jax.ShapeDtypeStruct((3,), f32),
        ),
        in_specs=[VMEM, VMEM],
        out_specs=(VMEM, VMEM, SMEM),
        compiler_params=params(),
        name="settle",
    )(everywhere(peak), state)
    gathered = lax.all_to_all(copies, "draw", 0, 0, tiled=True)
    jacobian = pl.pallas_call(
        lambda *refs: final_kernel(own, *refs),
        out_shape=jax.ShapeDtypeStruct((own, slots, slots), f32),
        in_specs=[SMEM, VMEM, VMEM],
        out_specs=VMEM,
        scratch_shapes=[pltpu.VMEM((8, 128), f32), pltpu.VMEM((2, 128, span * draw_count), jnp.bfloat16)],
        compiler_params=params(),
        cost_estimate=pl.CostEstimate(flops=2_000_000_000, bytes_accessed=8_000_000, transcendentals=0),
        name="final",
    )(counts, mean_own, raised)
    mean_util = gathered[:, :own, :slots].reshape(markets, slots)
    return (mean_util, jacobian, norms)


def solution(mesh):
    return jax.shard_map(
        shards,
        mesh=mesh,
        in_specs=(P("mkt", None, None), P("mkt", None, "draw"), P(), P("mkt", None), P("mkt")),
        out_specs=(P("mkt", None), P(("mkt", "draw"), None, None), P()),
        check_vma=False,
    )
```

time: 203 us -> 104 us (0.51)
  matrix products: 52.9 us -> 0 us
  blocking collectives: 44.3 us -> 80.8 us
  waiting for transfers between devices: 30.9 us -> 0.01 us
  other arithmetic: 18.7 us -> 0 us
  between operations: 16.5 us -> 0.69 us
  starting transfers between devices: 18.9 us -> 3.74 us
  local copies, waits for them, and re-layouts: 18.6 us -> 6.15 us
  Pallas kernels: 0 us -> 11.8 us
    dot_general x30 -> x0, matrix products: 52.9 us -> none  [the longest x24 47 us: market_terms(): jnp.einsum('mjk,mkr->mjr', scaled, nu_draws, precision=lax.Precision.HIGH...]
    all_to_all x3 -> x4, blocking collectives: 29.3 us -> 80.8 us  [the longest x3 62 us: everywhere(): lax.all_to_all(peak.reshape(every, 1, 128), EVERY, 0, 0, tiled=True)]
    all_to_all x3 -> x1, waiting for transfers between devices: 25.5 us -> 0.01 us  [shards(): gathered = lax.all_to_all(copies, 'draw', 0, 0, tiled=True)]
    all_to_all x3 -> x1, starting transfers between devices: 18.9 us -> 3.74 us  [shards(): gathered = lax.all_to_all(copies, 'draw', 0, 0, tiled=True)]
    all_gather x1 -> x0, blocking collectives: 15 us -> none  [total_of_pieces(): return lax.all_gather(shard, axis).sum(0)]
    pallas_call x0 -> x5, Pallas kernels: none -> 11.8 us  [the longest x1 5.32 us: shards(): pl.pallas_call(lambda *refs: final_kernel(own, *refs), out_shape=jax.Shap...]
    gather x3 -> x0, local copies, waits for them, and re-layouts: 9.73 us -> none  [the longest x1 5.54 us: unpack_cross(): whole = jnp.take(packed, jnp.asarray(lookup_table.reshape(-1)), axis=1)]
    reduce_sum x30 -> x0, other arithmetic: 6.35 us -> none  [the longest x24 3.46 us: market_terms(): shares = jnp.sum(chance, axis=2) * inverse]
  transfers between devices with their start and end apart: 4 -> 1, of which waited for: 4 -> 0; matrix products, arithmetic and copies ran while one was open for 1% -> 0% of each run, Pallas kernels for 0% -> 5%
where the time goes in v1:
time: 104 us; the launch traced here: 103 us
  blocking collectives  80.8 us (78%)
  Pallas kernels  11.8 us (11%)
  local copies, waits for them, and re-layouts  6.15 us (6%)
  starting transfers between devices  3.74 us (4%)
    all_to_all x3, blocking collectives, everywhere(): lax.all_to_all(peak.reshape(every, 1, 128), EVERY, 0, 0, tiled=True)  62 us
    all_to_all x1, blocking collectives, shards(): nu_own = lax.all_to_all(nu_draws, 'draw', 0, 0, tiled=True)  18.8 us
    unnamed x14, local copies, waits for them, and re-layouts  5.54 us
    pallas_call x1, Pallas kernels, shards(): pl.pallas_call(lambda *refs: final_kernel(own, *refs), out_shape=jax.Shap...  5.32 us
    all_to_all x1, starting transfers between devices, shards(): gathered = lax.all_to_all(copies, 'draw', 0, 0, tiled=True)  3.74 us
    pallas_call x2, Pallas kernels, shards(): pl.pallas_call(lambda *refs, turn=turn: next_kernel(own, turn, *refs), ou...  3.06 us
    pallas_call x1, Pallas kernels, shards(): pl.pallas_call(lambda *refs: start_kernel(own, *refs), out_shape=(raised_...  2.58 us
  transfers between devices with their start and end apart: 1, of which 0 were waited for; matrix products, arithmetic and copies ran while one was open for 0% of the time, Pallas kernels for 5%

profile of v1, /device:TPU:1, one launch (start us, length us, event | category | flops | bytes accessed | tf_op | source)
XLA Modules:
  0.0 103.2 jit_solution(9975454520314480894)
XLA Ops:
  0.6 18.8 %all_to_all.25.refs_4_ = f32[48,8,512]{2,1,0:T(8,128)S(1)} all-to-all(f32[48,8,512]{2,1,0:T(8,128)} %param.6), channel_id=1, replica_groups=mesh['mkt'=32,'draw'=8] {'draw'}, dimensions={0} | all-to-all | bytes 1572864 | tf_op jit(solution)/shard_map/all_to_all | solution.py:188
  19.4 0.0 copy-start.2
  19.4 0.9 copy-done.2
  20.3 0.0 copy-start.3
  20.3 0.7 copy-done.3
  21.1 0.0 copy-start.4
  21.1 0.7 copy-done.4
  21.7 0.0 copy-start.5
  21.7 0.7 copy-done.5
  22.4 2.6 %start.1 = (f32[6,56,4096]{2,1,0:T(8,128)S(1)}, f32[5,56,8]{2,1,0:T(8,128)S(1)}, f32[256,128]{1,0:T(8,128)S(1)}) custom-call(s32[48]{0:T(128)S(1)} %copy-done.5, f32[8]{0:T(128)S(1)} %copy-done.4, f32[48,56]{1,0:T(8,128)S(1)} %copy-done.3, f32[48,8,56]{2,1,0:T(8,128)S(1)} %bitcast.17, f32[48,8,512]{2,1,0:T(8,128)S(1)} %all_to_all.25.refs_4_), custom_call_target="tpu_custom_call" | custom-call | tf_op jit(solution)/shard_map/start/pallas_call | solution.py:189
  25.0 0.0 copy-start
  25.0 25.3 %all_to_all.26 = f32[256,1,128]{2,1,0:T(1,128)S(1)} all-to-all(f32[256,1,128]{2,1,0:T(1,128)S(1)} %bitcast.18), channel_id=1, replica_groups=mesh['mkt'=32,'draw'=8] {'mkt','draw'}, dimensions={0} | all-to-all | bytes 262144 | tf_op jit(solution)/shard_map/all_to_all | solution.py:186
  50.3 0.0 copy-start.6
  50.3 1.5 %next.2 = (f32[5,56,8]{2,1,0:T(8,128)S(1)}, f32[256,128]{1,0:T(8,128)S(1)}) custom-call(f32[256,128]{1,0:T(8,128)S(1)} %bitcast.14, f32[5,56,8]{2,1,0:T(8,128)S(1)} %get-tuple-element.14.refs_1_, f32[6,56,4096]{2,1,0:T(8,128)S(1)} %get-tuple-element.15.refs_2_), custom_call_target="tpu_custom_call" | custom-call | tf_op jit(solution)/shard_map/next/pallas_call | solution.py:199
  51.8 18.4 %all_to_all.27 = f32[256,1,128]{2,1,0:T(1,128)S(1)} all-to-all(f32[256,1,128]{2,1,0:T(1,128)S(1)} %bitcast.19), channel_id=1, replica_groups=mesh['mkt'=32,'draw'=8] {'mkt','draw'}, dimensions={0} | all-to-all | bytes 262144 | tf_op jit(solution)/shard_map/all_to_all | solution.py:186
  70.2 1.5 %next.3 = (f32[5,56,8]{2,1,0:T(8,128)S(1)}, f32[256,128]{1,0:T(8,128)S(1)}) custom-call(f32[256,128]{1,0:T(8,128)S(1)} %bitcast.15, f32[5,56,8]{2,1,0:T(8,128)S(1)} %get-tuple-element.17.refs_1_, f32[6,56,4096]{2,1,0:T(8,128)S(1)} %get-tuple-element.15.refs_2_), custom_call_target="tpu_custom_call" | custom-call | tf_op jit(solution)/shard_map/next/pallas_call | solution.py:199
  71.7 0.0 copy-done
  71.7 18.4 %all_to_all.28 = f32[256,1,128]{2,1,0:T(1,128)S(1)} all-to-all(f32[256,1,128]{2,1,0:T(1,128)S(1)} %bitcast.20), channel_id=1, replica_groups=mesh['mkt'=32,'draw'=8] {'mkt','draw'}, dimensions={0} | all-to-all | bytes 262144 | tf_op jit(solution)/shard_map/all_to_all | solution.py:186
  90.1 0.9 settle.1
  91.0 3.7 %all-to-all-start.4 = ((f32[8,8,128]{2,1,0:T(8,128)}), f32[8,8,128]{2,1,0:T(8,128)S(1)}, u32[]{:S(2)}, u32[]{:S(2)}) async-start(f32[8,8,128]{2,1,0:T(8,128)} %get-tuple-element.20), calls=%async_computation.4 | async-start | bytes 65536 | tf_op jit(solution)/shard_map/all_to_all | solution.py:219
  94.7 0.0 copy-done.6
  94.7 0.0 copy-start.1
  94.7 2.6 %copy-done.1 = f32[6,56,4096]{2,1,0:T(8,128)S(1)} copy-done((f32[6,56,4096]{2,1,0:T(8,128)S(1)}, f32[6,56,4096]{2,1,0:T(8,128)}, u32[]{:S(2)}) %copy-start.1) | copy-done | bytes 5505048
  97.3 5.3 %final.1 = f32[6,56,56]{2,1,0:T(8,128)} custom-call(s32[48]{0:T(128)S(1)} %copy-done.6, f32[56,8]{1,0:T(8,128)S(1)} %get-tuple-element.21.refs_1_, f32[6,56,4096]{2,1,0:T(8,128)S(1)} %copy-done.1), custom_call_target="tpu_custom_call" | custom-call | flops 2000000000 | bytes 8000000 | tf_op jit(solution)/shard_map/final/pallas_call | solution.py:220
  102.6 0.0 all-to-all-done.4
  102.6 0.6 reshape.33
Async XLA Ops:
  19.4 0.9 copy-start.2
  20.3 0.7 copy-start.3
  21.1 0.7 copy-start.4
  21.7 0.7 copy-start.5
  25.0 46.7 %copy-start = (f32[6,56,4096]{2,1,0:T(8,128)}, f32[6,56,4096]{2,1,0:T(8,128)S(1)}, u32[]{:S(2)}) copy-start(f32[6,56,4096]{2,1,0:T(8,128)S(1)} %get-tuple-element.15.refs_2_) | copy-start | bytes 16515076
  50.3 44.4 %copy-start.6 = (s32[48]{0:T(128)S(1)}, s32[48]{0:T(128)}, u32[]{:S(2)}) copy-start(s32[48]{0:T(128)} %refs_0_.3) | copy-start | bytes 580
  91.0 11.6 %all-to-all-start.4 = ((f32[8,8,128]{2,1,0:T(8,128)}), f32[8,8,128]{2,1,0:T(8,128)S(1)}, u32[]{:S(2)}, u32[]{:S(2)}) async-start(f32[8,8,128]{2,1,0:T(8,128)} %get-tuple-element.20), calls=%async_computation.4 | async-start | bytes 65536 | tf_op jit(solution)/shard_map/all_to_all | solution.py:219
  94.7 2.6 %copy-start.1 = (f32[6,56,4096]{2,1,0:T(8,128)S(1)}, f32[6,56,4096]{2,1,0:T(8,128)}, u32[]{:S(2)}) copy-start(f32[6,56,4096]{2,1,0:T(8,128)} %copy-done) | copy-start | bytes 16515076
